TPU v7x, 768 devices: a whole 4x8x12 slice. The times are simulated.
768 devices in a mesh: dp: 32 (over x, z_hi, core), mp: 24 (over z_lo, y).
Axes of the slice: x: 4, y: 8, z: 12 (z_hi: 4, z_lo: 3; z = z_hi * 3 + z_lo), core: 2. Of those that a mesh axis runs over, the one named last changes fastest.
Arguments:
- image_tokens: bfloat16 [3072, 32, 1152], P('dp'), may hold values from -6 to 6
- image_counts: int32 [32, 24], P('dp'), may hold values from 2 to 4, as said below
- image_ids: int32 [3072], P('dp'), may hold values from 0 to 767
- norm_gain: float32 [1152], replicated, may hold values from 0.1 to 1.9
- norm_bias: float32 [1152], replicated, may hold values from -3 to 3
- up_weight: bfloat16 [1152, 3072], P(None, 'mp'), may hold values from -0.1875 to 0.1875
- down_weight: bfloat16 [3072, 1152], P('mp'), may hold values from -0.109375 to 0.109375
- text_rows: bfloat16 [3072, 1152], P(('dp', 'mp')), may hold values from -6 to 6
- text_counts: int32 [768], P(('dp', 'mp')), may hold values from 2 to 4, as said below
- text_ids: int32 [3072], replicated, may hold values from 0 to 767
- logit_scale: float32 [1], replicated, may hold values from 30 to 45
- logit_bias: float32 [1], replicated, may hold values from -8 to -5.5
Outputs:
- text_grad: float32 [3072, 1152], P(('dp', 'mp'))
Inputs may be any that keep to these rules, and one draw needn't show every extreme that they name: `image_counts`: entries count the valid rows among the 4 padded rows of one device's block; in every draw some block has all 4 rows valid. `text_counts`: entries count the valid rows among the 4 padded rows of one device's block; in every draw some block has all 4 rows valid.
All inputs are finite; a program needn't handle non-finite values.
Results may differ from a plain program's by a relative error of at most 0.02.
Values may be sent and summed in bfloat16 or wider, within the bound.
A program may use at most 32 MiB of HBM per device.

v0:
```python
import jax
import jax.numpy as jnp
from jax import lax
from jax.sharding import PartitionSpec as P

norm_eps = 1e-06


def in_blocks(shard, dim, count):
    before, after = (shard.shape[:dim], shard.shape[dim + 1 :])
    return jnp.moveaxis(shard.reshape(*before, count, -1, *after), dim, 0)


def sum_at_owner(shard, axis, dim):
    count = lax.axis_size(axis)
    tiles = lax.all_to_all(in_blocks(shard, dim, count), axis, 0, 0, tiled=True)
    return jnp.sum(tiles.astype(jnp.float32), axis=0)


def laid_out(tiles, dim):
    shape = list(tiles.shape[1:])
    shape[dim] *= tiles.shape[0]
    return jnp.moveaxis(tiles, 0, dim).reshape(shape)


def copy_for_each(shard, axis):
    count = lax.axis_size(axis)
    return lax.all_to_all(
        jnp.broadcast_to(shard[None], (count, *shard.shape)), axis, 0, 0, tiled=True
    )


def gather_directly(shard, axis, dim):
    return laid_out(copy_for_each(shard, axis), dim)


def layer_norm(row_values, gain_row, shift_row):
    values = row_values.astype(jnp.float32)
    center = jnp.mean(values, axis=-1, keepdims=True)
    spread = jnp.mean(jnp.square(values - center), axis=-1, keepdims=True)
    return (values - center) * lax.rsqrt(spread + norm_eps) * gain_row + shift_row


def unit_rows(values):
    return values * lax.rsqrt(jnp.sum(values * values, axis=-1, keepdims=True) + norm_eps)


def pair_terms(text_block, block_ids, image_emb, image_ids, image_valid, logit_mul, logit_add):
    cosines = lax.dot_general(
        text_block, image_emb, (((1,), (1,)), ((), ())), preferred_element_type=jnp.float32
    )
    logits = logit_mul * cosines + logit_add
    sign_table = jnp.where(block_ids[:, None] == image_ids[None, :], 1.0, -1.0).astype(jnp.float32)
    margin = -sign_table * logits
    weights = (image_valid[None, :] * -sign_table * jax.nn.sigmoid(margin) * logit_mul).astype(
        jnp.bfloat16
    )
    return jnp.dot(weights, image_emb, preferred_element_type=jnp.float32)


def local(
    image_tokens,
    image_counts,
    image_ids,
    norm_gain,
    norm_bias,
    up_weight,
    down_weight,
    text_rows,
    text_counts,
    text_ids,
    logit_scale,
    logit_bias,
):
    width_shards = lax.axis_size("mp")
    data_shards = lax.axis_size("dp")
    width_index = lax.axis_index("mp")
    rows_dev = text_rows.shape[0]
    group_rows = image_tokens.shape[0]
    normed = layer_norm(image_tokens, norm_gain, norm_bias).astype(jnp.bfloat16)
    hidden = jax.nn.gelu(jnp.dot(normed, up_weight, preferred_element_type=jnp.float32)).astype(
        jnp.bfloat16
    )
    pooled_hidden = jnp.mean(hidden.astype(jnp.float32), axis=1).astype(jnp.bfloat16)
    own_start = width_index * rows_dev
    own_tokens = lax.dynamic_slice_in_dim(image_tokens, own_start, rows_dev, 0)
    pooled_tokens = jnp.mean(own_tokens.astype(jnp.float32), axis=1)
    tower_out = pooled_tokens + sum_at_owner(
        jnp.dot(pooled_hidden, down_weight, preferred_element_type=jnp.float32).astype(
            jnp.bfloat16
        ),
        "mp",
        0,
    )
    own_emb = unit_rows(tower_out).astype(jnp.bfloat16)
    image_emb = gather_directly(own_emb, "mp", 0)
    slot_index = jnp.arange(group_rows, dtype=jnp.int32) % rows_dev
    image_valid = (
        slot_index < jnp.repeat(image_counts[0], rows_dev, total_repeat_length=group_rows)
    ).astype(jnp.float32)
    text_valid = (jnp.arange(rows_dev, dtype=jnp.int32) < text_counts[0]).astype(jnp.float32)
    text_emb = unit_rows(text_rows.astype(jnp.float32)).astype(jnp.bfloat16)
    logit_mul = logit_scale[0]
    logit_add = logit_bias[0]
    every_text = gather_directly(text_emb, "dp", 0)
    id_table = text_ids.reshape(data_shards, width_shards * rows_dev)
    every_ids = lax.dynamic_slice_in_dim(id_table, width_index * rows_dev, rows_dev, 1).reshape(-1)
    grad_rows = pair_terms(
        every_text, every_ids, image_emb, image_ids, image_valid, logit_mul, logit_add
    )
    text_grad = sum_at_owner(grad_rows.astype(jnp.bfloat16), "dp", 0)
    return text_grad * text_valid[:, None]


def solution(mesh):
    placed = (
        P("dp", None, None),
        P("dp", None),
        P("dp"),
        P(),
        P(),
        P(None, "mp"),
        P("mp", None),
        P(("dp", "mp"), None),
        P(("dp", "mp")),
        P(),
        P(),
        P(),
    )
    return jax.shard_map(
        local, mesh=mesh, in_specs=placed, out_specs=P(("dp", "mp"), None), check_vma=False
    )
```

profile of v0, /device:TPU:1, one launch (start us, length us, event | category | flops | bytes accessed | tf_op | source)
XLA Modules:
  0.0 111.4 jit_solution(4155167484836413916)
XLA Ops:
  0.0 4.2 %convert_reduce_fusion = f32[96,32]{1,0:T(8,128)S(1)} fusion(bf16[96,32,1152]{2,1,0:T(8,128)(2,1)} %param.14), kind=kLoop, calls=%fused_computation.2 | loop fusion | flops 7074816 | bytes 7090176 | tf_op jit(solution)/shard_map/reduce_sum | solution.py:39
  4.2 0.9 copy-done.2
  5.1 2.0 %fusion.2 = f32[96,32]{1,0:T(8,128)S(1)} fusion(bf16[96,32,1152]{2,1,0:T(8,128)(2,1)S(1)} %copy-done.2, f32[96,32]{1,0:T(8,128)S(1)} %broadcast_multiply_fusion), kind=kLoop, calls=%fused_computation.5 | loop fusion | flops 14152704 | bytes 7102464 | tf_op jit(solution)/shard_map/reduce_sum | solution.py:40
  7.2 3.7 %convert_reduce_fusion.1 = f32[96,128]{1,0:T(8,128)S(1)} fusion(bf16[96,32,1152]{2,1,0:T(8,128)(2,1)S(1)} %copy-done.2, f32[1152]{0:T(1024)S(1)} %copy-done.8, f32[1152]{0:T(1024)S(1)} %copy-done.9, f32[96,32]{1,0:T(8,128)S(1)} %add_rsqrt_fusion, f32[96,32]{1,0:T(8,128)S(1)} %broadcast_multiply_fusion, bf16[1152,128]{1,0:T(8,128)(2,1)S(1)} %copy-done.7), kind=kOutput, calls=%fused_computation.21 | convolution fusion | flops 931516416 | bytes 7455744 | tf_op jit(solution)/shard_map/dot_general | solution.py:81
  11.0 0.2 convolution_convert_fusion.1
  11.2 0.7 reshape.120
  11.9 11.5 %all-to-all-start.1 = ((bf16[24,4,1152]{2,1,0:T(4,128)(2,1)}), bf16[24,4,1152]{2,1,0:T(4,128)(2,1)S(1)}, u32[]{:S(2)}, u32[]{:S(2)}) async-start(bf16[24,4,1152]{2,1,0:T(4,128)(2,1)} %reshape.120), calls=%async_computation.1 | async-start | bytes 442368 | tf_op jit(solution)/shard_map/all_to_all | solution.py:16
  23.4 1.0 convert_reduce_fusion.3
  24.5 0.1 fusion.42
  24.6 0.1 fusion.43
  24.7 7.9 %all-to-all-done.1 = bf16[24,4,1152]{2,1,0:T(4,128)(2,1)S(1)} async-done(((bf16[24,4,1152]{2,1,0:T(4,128)(2,1)}), bf16[24,4,1152]{2,1,0:T(4,128)(2,1)S(1)}, u32[]{:S(2)}, u32[]{:S(2)}) %all-to-all-start.1) | async-done | bytes 221216 | tf_op jit(solution)/shard_map/all_to_all | solution.py:16
  32.6 0.8 broadcast_in_dim.16
  33.4 19.2 %all-to-all-start = ((bf16[32,4,1152]{2,1,0:T(4,128)(2,1)}), bf16[32,4,1152]{2,1,0:T(4,128)(2,1)S(1)}, u32[]{:S(2)}, u32[]{:S(2)}) async-start(bf16[32,4,1152]{2,1,0:T(4,128)(2,1)} %broadcast_in_dim.16), calls=%async_computation | async-start | bytes 589824 | tf_op jit(solution)/shard_map/all_to_all | solution.py:28
  52.6 0.1 convert_reduce_fusion.4
  52.7 0.1 multiply_reduce_fusion
  52.9 0.1 multiply_convert_fusion.2
  52.9 15.8 %all-to-all-done = bf16[32,4,1152]{2,1,0:T(4,128)(2,1)S(1)} async-done(((bf16[32,4,1152]{2,1,0:T(4,128)(2,1)}), bf16[32,4,1152]{2,1,0:T(4,128)(2,1)S(1)}, u32[]{:S(2)}, u32[]{:S(2)}) %all-to-all-start) | async-done | bytes 294944 | tf_op jit(solution)/shard_map/all_to_all | solution.py:28
  68.7 0.7 broadcast_in_dim.17
  69.5 6.7 %all-to-all-start.2 = ((bf16[24,4,1152]{2,1,0:T(4,128)(2,1)}), bf16[24,4,1152]{2,1,0:T(4,128)(2,1)S(1)}, u32[]{:S(2)}, u32[]{:S(2)}) async-start(bf16[24,4,1152]{2,1,0:T(4,128)(2,1)} %broadcast_in_dim.17), calls=%async_computation.2 | async-start | bytes 442368 | tf_op jit(solution)/shard_map/all_to_all | solution.py:28
  76.1 0.1 reshape.118
  76.2 0.1 constant_dynamic-slice_fusion
  76.3 0.1 eq.17
  77.7 1.2 %gather_fusion = s32[96]{0:T(128)S(1)} fusion(s32[24]{0:T(128)S(1)} %bitcast.14, s32[1024]{0:T(1024)S(1)} %pad_clamp_fusion), kind=kCustom, calls=%fused_computation | custom fusion | bytes 1152 | tf_op jit(solution)/shard_map/jit(_take)/gather | solution.py:99
  79.0 0.1 reshape.119
  79.1 6.4 %all-to-all-done.2 = bf16[24,4,1152]{2,1,0:T(4,128)(2,1)S(1)} async-done(((bf16[24,4,1152]{2,1,0:T(4,128)(2,1)}), bf16[24,4,1152]{2,1,0:T(4,128)(2,1)S(1)}, u32[]{:S(2)}, u32[]{:S(2)}) %all-to-all-start.2) | async-done | bytes 221216 | tf_op jit(solution)/shard_map/all_to_all | solution.py:28
  85.4 0.1 reshape.121
  85.5 0.6 convolution_convert_fusion
  86.1 0.8 reshape.122
  86.9 7.6 %all-to-all-start.3 = ((bf16[32,4,1152]{2,1,0:T(4,128)(2,1)}), bf16[32,4,1152]{2,1,0:T(4,128)(2,1)S(1)}, u32[]{:S(2)}, u32[]{:S(2)}) async-start(bf16[32,4,1152]{2,1,0:T(4,128)(2,1)} %reshape.122), calls=%async_computation.3 | async-start | bytes 589824 | tf_op jit(solution)/shard_map/all_to_all | solution.py:16
  95.1 15.5 %all-to-all-done.3 = bf16[32,4,1152]{2,1,0:T(4,128)(2,1)S(1)} async-done(((bf16[32,4,1152]{2,1,0:T(4,128)(2,1)}), bf16[32,4,1152]{2,1,0:T(4,128)(2,1)S(1)}, u32[]{:S(2)}, u32[]{:S(2)}) %all-to-all-start.3) | async-done | bytes 294944 | tf_op jit(solution)/shard_map/all_to_all | solution.py:16
  110.6 0.1 convert_reduce_fusion.2
  110.7 0.7 broadcast_multiply_fusion.1
  (26 shorter events, 0.1 us)
Async XLA Ops:
  0.0 11.0 %copy-start = (bf16[128,1152]{1,0:T(8,128)(2,1)S(1)}, bf16[128,1152]{1,0:T(8,128)(2,1)}, u32[]{:S(2)}) copy-start(bf16[128,1152]{1,0:T(8,128)(2,1)} %param.20) | copy-start | bytes 884740
  0.0 5.1 %copy-start.2 = (bf16[96,32,1152]{2,1,0:T(8,128)(2,1)S(1)}, bf16[96,32,1152]{2,1,0:T(8,128)(2,1)}, u32[]{:S(2)}) copy-start(bf16[96,32,1152]{2,1,0:T(8,128)(2,1)} %param.14) | copy-start | bytes 21233668
  0.0 7.1 %copy-start.9 = (f32[1152]{0:T(1024)S(1)}, f32[1152]{0:T(1024)}, u32[]{:S(2)}) copy-start(f32[1152]{0:T(1024)} %param.17) | copy-start | bytes 13828
  0.0 7.1 %copy-start.8 = (f32[1152]{0:T(1024)S(1)}, f32[1152]{0:T(1024)}, u32[]{:S(2)}) copy-start(f32[1152]{0:T(1024)} %param.18) | copy-start | bytes 13828
  0.0 7.1 %copy-start.7 = (bf16[1152,128]{1,0:T(8,128)(2,1)S(1)}, bf16[1152,128]{1,0:T(8,128)(2,1)}, u32[]{:S(2)}) copy-start(bf16[1152,128]{1,0:T(8,128)(2,1)} %param.19) | copy-start | bytes 884740
  7.2 17.3 %copy-start.3 = (bf16[4,1152]{1,0:T(4,128)(2,1)S(1)}, bf16[4,1152]{1,0:T(4,128)(2,1)}, u32[]{:S(2)}) copy-start(bf16[4,1152]{1,0:T(4,128)(2,1)} %param.21) | copy-start | bytes 27652
  7.2 69.0 %copy-start.4 = (s32[3072]{0:T(1024)S(1)}, s32[3072]{0:T(1024)}, u32[]{:S(2)}) copy-start(s32[3072]{0:T(1024)} %param.23) | copy-start | bytes 36868
  7.2 70.5 %copy-start.6 = (s32[96]{0:T(128)S(1)}, s32[96]{0:T(128)}, u32[]{:S(2)}) copy-start(s32[96]{0:T(128)} %constant.130) | copy-start | bytes 1156
  7.2 70.5 %copy-start.1 = (s32[1,24]{1,0:T(1,128)S(1)}, s32[1,24]{1,0:T(1,128)}, u32[]{:S(2)}) copy-start(s32[1,24]{1,0:T(1,128)} %param.15) | copy-start | bytes 292
  7.2 78.3 %copy-start.5 = (s32[96]{0:T(128)S(1)}, s32[96]{0:T(128)}, u32[]{:S(2)}) copy-start(s32[96]{0:T(128)} %param.16) | copy-start | bytes 1156
  11.9 20.7 %all-to-all-start.1 = ((bf16[24,4,1152]{2,1,0:T(4,128)(2,1)}), bf16[24,4,1152]{2,1,0:T(4,128)(2,1)S(1)}, u32[]{:S(2)}, u32[]{:S(2)}) async-start(bf16[24,4,1152]{2,1,0:T(4,128)(2,1)} %reshape.120), calls=%async_computation.1 | async-start | bytes 442368 | tf_op jit(solution)/shard_map/all_to_all | solution.py:16
  33.4 35.3 %all-to-all-start = ((bf16[32,4,1152]{2,1,0:T(4,128)(2,1)}), bf16[32,4,1152]{2,1,0:T(4,128)(2,1)S(1)}, u32[]{:S(2)}, u32[]{:S(2)}) async-start(bf16[32,4,1152]{2,1,0:T(4,128)(2,1)} %broadcast_in_dim.16), calls=%async_computation | async-start | bytes 589824 | tf_op jit(solution)/shard_map/all_to_all | solution.py:28
  69.5 16.0 %all-to-all-start.2 = ((bf16[24,4,1152]{2,1,0:T(4,128)(2,1)}), bf16[24,4,1152]{2,1,0:T(4,128)(2,1)S(1)}, u32[]{:S(2)}, u32[]{:S(2)}) async-start(bf16[24,4,1152]{2,1,0:T(4,128)(2,1)} %broadcast_in_dim.17), calls=%async_computation.2 | async-start | bytes 442368 | tf_op jit(solution)/shard_map/all_to_all | solution.py:28
  86.9 23.7 %all-to-all-start.3 = ((bf16[32,4,1152]{2,1,0:T(4,128)(2,1)}), bf16[32,4,1152]{2,1,0:T(4,128)(2,1)S(1)}, u32[]{:S(2)}, u32[]{:S(2)}) async-start(bf16[32,4,1152]{2,1,0:T(4,128)(2,1)} %reshape.122), calls=%async_computation.3 | async-start | bytes 589824 | tf_op jit(solution)/shard_map/all_to_all | solution.py:16
where the time goes:
time: 112 us; the launch traced here: 111 us
  waiting for transfers between devices  45.6 us (41%)
  starting transfers between devices  44.9 us (40%)
  other arithmetic  8.6 us (8%)
  local copies, waits for them, and re-layouts  5.57 us (5%)
  matrix products  4.54 us (4%)
  between operations  2.22 us (2%)
    all_to_all x2, starting transfers between devices, copy_for_each(): lax.all_to_all(jnp.broadcast_to(shard[None], (count, *shard.shape)), axis...  25.9 us
    all_to_all x2, waiting for transfers between devices, sum_at_owner(): tiles = lax.all_to_all(in_blocks(shard, dim, count), axis, 0, 0, tiled=True)  23.4 us
    all_to_all x2, waiting for transfers between devices, copy_for_each(): lax.all_to_all(jnp.broadcast_to(shard[None], (count, *shard.shape)), axis...  22.2 us
    all_to_all x2, starting transfers between devices, sum_at_owner(): tiles = lax.all_to_all(in_blocks(shard, dim, count), axis, 0, 0, tiled=True)  19.1 us
    reduce_sum x1, other arithmetic, layer_norm(): center = jnp.mean(values, axis=-1, keepdims=True)  4.15 us
    dot_general x1, matrix products, local(): jnp.dot(normed, up_weight, preferred_element_type=jnp.float32)  3.72 us
  transfers between devices with their start and end apart: 4, of which 4 were waited for; matrix products, arithmetic and copies ran while one was open for 3% of the time, Pallas kernels for 0%

commit v1 on v0

v1 whole, which is shorter than its diff:
```python
import functools

import jax
import jax.numpy as jnp
from jax import lax
from jax.experimental import pallas as pl
from jax.experimental.pallas import tpu as pltpu
from jax.sharding import PartitionSpec as P

MESH = pl.DeviceIdType.MESH
EPS = 1e-06
F32 = jnp.float32
BF16 = jnp.bfloat16
GEOMETRY = (4, 4, 3, 8)


def await_bytes(ref, sem):
    pltpu.make_async_copy(ref, ref, sem).wait()


def unit_rows(values):
    return values * lax.rsqrt(jnp.sum(values * values, axis=-1, keepdims=True) + EPS)


def y_offset(step, ny):
    half = (step + 1) // 2
    return ny // 2 + half * (1 - 2 * (step % 2))


def kernel(
    geometry,
    tokens,
    counts,
    image_ids,
    gain,
    shift,
    w_up,
    w_down,
    text_rows,
    text_ids,
    scale,
    bias,
    out,
    x_buf,
    counts_v,
    ids_v,
    gain_v,
    shift_v,
    up_v,
    down_v,
    text_v,
    text_ids_s,
    scale_v,
    bias_v,
    w_aug,
    w_sum,
    w_shift,
    part_send,
    part_recv,
    own_part,
    emb_own,
    emb_peer,
    meta_own,
    meta_peer,
    text_all,
    rows_f32,
    grad_send,
    grad_recv,
    own_grad,
    in_sem,
    x_sem,
    part_send_sem,
    part_recv_sem,
    emb_send_sem,
    emb_recv_sem,
    pair_send_sem,
    pair_recv_sem,
    meta_send_sem,
    meta_recv_sem,
    text_send_sem,
    text_recv_sem,
    grad_send_sem,
    grad_recv_sem,
):
    nx, nzh, nzl, ny = geometry
    width = nzl * ny
    chips = nx * nzh
    rows, d = text_rows.shape
    patches = tokens.shape[1]
    units = w_up.shape[1]
    group = width * rows
    lanes = d // 128
    dp = lax.axis_index("dp")
    mp = lax.axis_index("mp")
    core = dp % 2
    my_x = dp // (2 * nzh)
    my_zh = (dp // 2) % nzh
    my_zl = mp // ny
    my_y = mp % ny
    partner = dp + 1 - 2 * core

    def mp_of(y_off, z_off):
        return ((my_zl + z_off) % nzl) * ny + (my_y + y_off) % ny

    def dp_of(x_off, z_off):
        return (((my_x + x_off) % nx) * nzh + (my_zh + z_off) % nzh) * 2 + core

    mp_partners = [
        (y_off, z_off)
        for y_off in [y_offset(s, ny) for s in range(ny)]
        for z_off in [(z + 1) % nzl for z in range(nzl)]
    ][:-1]
    z_order = sorted(range(nzh), key=lambda o: -min(o, nzh - o))
    x_order = sorted(range(nx), key=lambda o: -min(o, nx - o))
    dp_partners = [(x_off, z_off) for z_off in z_order for x_off in x_order][:-1]

    barrier = pltpu.get_barrier_semaphore()
    for y_off, z_off in mp_partners:
        pl.semaphore_signal(barrier, inc=1, device_id=(dp, mp_of(y_off, z_off)), device_id_type=MESH)
    for x_off, z_off in dp_partners:
        pl.semaphore_signal(barrier, inc=1, device_id=(dp_of(x_off, z_off), mp), device_id_type=MESH)
    pl.semaphore_signal(barrier, inc=1, device_id=(partner, mp), device_id_type=MESH)

    small = [
        (w_up, up_v),
        (gain, gain_v),
        (shift, shift_v),
        (w_down, down_v),
        (text_rows, text_v),
        (counts, counts_v),
        (image_ids, ids_v),
        (text_ids, text_ids_s),
        (scale, scale_v),
        (bias, bias_v),
    ]
    for index, (source, target) in enumerate(small[:3]):
        pltpu.make_async_copy(source, target, in_sem.at[index]).start()

    def load(step, z_off):
        start = mp_of(y_offset(step, ny), z_off) * rows
        pltpu.make_async_copy(
            tokens.at[pl.ds(start, rows)], x_buf.at[step, pl.ds(z_off * rows, rows)], x_sem.at[step]
        ).start()

    for step in range(ny):
        for z_off in range(nzl):
            load(step, z_off)
        if step == 0:
            for index, (source, target) in enumerate(small):
                if index >= 3:
                    pltpu.make_async_copy(source, target, in_sem.at[index]).start()

    for index in range(3):
        pltpu.make_async_copy(*small[index], in_sem.at[index]).wait()

    total = jnp.zeros((1, units), F32)
    moved = jnp.zeros((1, units), F32)
    for j in range(lanes):
        cut = pl.ds(j * 128, 128)
        block = up_v[cut, :].astype(F32)
        gain_column = jnp.transpose(jnp.broadcast_to(gain_v[:, cut], (128, 128)))[:, :1]
        shift_column = jnp.transpose(jnp.broadcast_to(shift_v[:, cut], (128, 128)))[:, :1]
        scaled = (block * gain_column).astype(BF16)
        w_aug[cut, pl.ds(0, units)] = scaled
        w_aug[cut, pl.ds(units, 128)] = jnp.ones((128, 128), BF16)
        total += jnp.sum(scaled.astype(F32), axis=0, keepdims=True)
        moved += jnp.sum(block * shift_column, axis=0, keepdims=True)
    w_sum[...] = total
    w_shift[...] = moved

    for index in range(3, len(small)):
        pltpu.make_async_copy(*small[index], in_sem.at[index]).wait()

    my_chip = dp // 2
    text_all[my_chip] = unit_rows(text_v[...].astype(F32)).astype(BF16)
    slot = lax.broadcasted_iota(jnp.int32, (width, group), 1)
    owner = lax.broadcasted_iota(jnp.int32, (width, group), 0)
    spread = jnp.where(slot // rows == owner, 1.0, 0.0).astype(BF16)
    row_counts = jnp.dot(
        jnp.broadcast_to(counts_v[...].astype(F32), (8, width)).astype(BF16),
        spread,
        preferred_element_type=F32,
    )[:1]
    place = (lax.broadcasted_iota(jnp.int32, (1, group), 1) % rows).astype(F32)
    meta_own[pl.ds(0, 1), pl.ds(0, group)] = ids_v[...].astype(F32)
    meta_own[pl.ds(1, 1), pl.ds(0, group)] = jnp.where(place < row_counts, 1.0, 0.0)

    pl.semaphore_wait(barrier, len(mp_partners) + len(dp_partners) + 1)

    meta_copy = pltpu.make_async_remote_copy(
        meta_own, meta_peer, meta_send_sem, meta_recv_sem, device_id=(partner, mp), device_id_type=MESH
    )
    meta_copy.start()
    for x_off, z_off in dp_partners:
        pltpu.make_async_remote_copy(
            text_all.at[my_chip],
            text_all.at[my_chip],
            text_send_sem,
            text_recv_sem,
            device_id=(dp_of(x_off, z_off), mp),
            device_id_type=MESH,
        ).start()

    def chunk(step, carry):
        await_bytes(x_buf.at[step], x_sem.at[step])
        images = nzl * rows
        count = images * patches
        x = x_buf[step].reshape(count, d)
        product = jnp.dot(x, w_aug[...], preferred_element_type=F32)
        mean = product[:, units:] * (1.0 / d)
        squares = jnp.zeros((count, 128), F32)
        for j in range(lanes):
            piece = x_buf[step, :, :, pl.ds(j * 128, 128)].reshape(count, 128).astype(F32) - mean
            squares += piece * piece
        spread_of = lax.rsqrt(jnp.sum(squares, axis=-1, keepdims=True) * (1.0 / d) + EPS)
        before = (product[:, :units] - mean * w_sum[...]) * spread_of + w_shift[...]
        hidden = jax.nn.gelu(before).astype(BF16).astype(F32)
        pooled = jnp.sum(hidden.reshape(images, patches, units), axis=1) * (1.0 / patches)
        part = jnp.dot(pooled.astype(BF16), down_v[...], preferred_element_type=F32)
        y_off = y_offset(step, ny)
        for z_off in [(z + 1) % nzl for z in range(nzl)]:
            term = part[z_off * rows : (z_off + 1) * rows]
            where_to = step * nzl + (z_off + nzl - 1) % nzl

            def send(term=term, where_to=where_to, z_off=z_off):
                part_send[where_to] = term.astype(BF16)
                pltpu.make_async_remote_copy(
                    part_send.at[where_to],
                    part_recv.at[where_to],
                    part_send_sem,
                    part_recv_sem,
                    device_id=(dp, mp_of(y_off, z_off)),
                    device_id_type=MESH,
                ).start()

            if z_off > 0:
                send()
            else:
                pl.when(step < ny - 1)(send)

                @pl.when(step == ny - 1)
                def _(term=term):
                    own_part[...] = term

        return carry

    lax.fori_loop(0, ny, chunk, 0)

    pooled_tokens = jnp.sum(x_buf[ny - 1, pl.ds(0, rows)].astype(F32), axis=1) * (1.0 / patches)
    tower = pooled_tokens + own_part[...]

    id_blocks = []
    lane_row = lax.broadcasted_iota(jnp.int32, (8, 128), 0)
    for start in range(0, chips * rows, 8):
        block = jnp.zeros((8, 128), jnp.int32)
        for k in range(8):
            chip, r = (start + k) // rows, (start + k) % rows
            entry = text_ids_s[((chip * 2 + core) * width + mp) * rows + r]
            block = jnp.where(lane_row == k, entry, block)
        id_blocks.append(block)
    id_column = jnp.concatenate(id_blocks, axis=0)[:, :group].astype(F32)

    await_bytes(part_recv, part_recv_sem)
    tower += jnp.sum(part_recv[...].astype(F32), axis=0)
    emb_own[mp] = unit_rows(tower).astype(BF16)
    for y_off, z_off in mp_partners:
        pltpu.make_async_remote_copy(
            emb_own.at[mp],
            emb_own.at[mp],
            emb_send_sem,
            emb_recv_sem,
            device_id=(dp, mp_of(y_off, z_off)),
            device_id_type=MESH,
        ).start()

    def flat(blocks_ref, count):
        for k in range(count):
            rows_f32[pl.ds(k * rows, rows), :] = blocks_ref[k].astype(F32)
        return rows_f32[pl.ds(0, count * rows), :].astype(BF16)

    await_bytes(text_all.at[pl.ds(0, chips - 1)], text_recv_sem)
    text_emb = flat(text_all, chips)
    meta_copy.wait_recv()

    def pair_terms(emb, meta):
        cosines = lax.dot_general(
            text_emb, emb, (((1,), (1,)), ((), ())), preferred_element_type=F32
        )
        logits = scale_v[...] * cosines + bias_v[...]
        same = id_column == meta[pl.ds(0, 1), pl.ds(0, group)]
        sign = jnp.where(same, 1.0, -1.0)
        weights = (
            meta[pl.ds(1, 1), pl.ds(0, group)] * -sign * jax.nn.sigmoid(-sign * logits) * scale_v[...]
        )
        return jnp.dot(weights.astype(BF16), emb, preferred_element_type=F32)

    await_bytes(emb_own.at[pl.ds(0, width - 1)], emb_recv_sem)
    pair_copy = pltpu.make_async_remote_copy(
        emb_own, emb_peer, pair_send_sem, pair_recv_sem, device_id=(partner, mp), device_id_type=MESH
    )
    pair_copy.start()
    grads = pair_terms(flat(emb_own, width), meta_own)
    pair_copy.wait_recv()
    grads += pair_terms(flat(emb_peer, width), meta_peer)

    for k in range(chips):
        grad_send[k] = grads[k * rows : (k + 1) * rows].astype(BF16)
    for index, (x_off, z_off) in enumerate(dp_partners):
        target = dp_of(x_off, z_off)
        pltpu.make_async_remote_copy(
            grad_send.at[target // 2],
            grad_recv.at[index],
            grad_send_sem,
            grad_recv_sem,
            device_id=(target, mp),
            device_id_type=MESH,
        ).start()
    own_grad[...] = grad_send[my_chip].astype(F32)

    await_bytes(part_send, part_send_sem)
    await_bytes(emb_own.at[pl.ds(0, width - 1)], emb_send_sem)
    await_bytes(text_all.at[pl.ds(0, chips - 1)], text_send_sem)
    meta_copy.wait_send()
    pair_copy.wait_send()
    await_bytes(grad_send.at[pl.ds(0, chips - 1)], grad_send_sem)
    await_bytes(grad_recv, grad_recv_sem)
    out[...] = own_grad[...] + jnp.sum(grad_recv[...].astype(F32), axis=0)


def fused(geometry, tokens, counts, image_ids, gain, shift, w_up, w_down, text_rows, text_ids, scale, bias):
    nx, nzh, nzl, ny = geometry
    width, chips = nzl * ny, nx * nzh
    rows, d = text_rows.shape
    units = w_up.shape[1]
    patches = tokens.shape[1]
    group = width * rows
    meta_lanes = -(-group // 128) * 128
    dma = pltpu.SemaphoreType.DMA
    return pl.pallas_call(
        functools.partial(kernel, geometry),
        out_shape=jax.ShapeDtypeStruct((rows, d), F32),
        in_specs=[pl.BlockSpec(memory_space=pl.ANY)] * 11,
        out_specs=pl.BlockSpec(memory_space=pltpu.VMEM),
        scratch_shapes=[
            pltpu.VMEM((ny, nzl * rows, patches, d), BF16),
            pltpu.VMEM(counts.shape, jnp.int32),
            pltpu.VMEM(image_ids.shape, jnp.int32),
            pltpu.VMEM(gain.shape, F32),
            pltpu.VMEM(shift.shape, F32),
            pltpu.VMEM(w_up.shape, BF16),
            pltpu.VMEM(w_down.shape, BF16),
            pltpu.VMEM(text_rows.shape, BF16),
            pltpu.SMEM(text_ids.shape, jnp.int32),
            pltpu.VMEM(scale.shape, F32),
            pltpu.VMEM(bias.shape, F32),
            pltpu.VMEM((d, units + 128), BF16),
            pltpu.VMEM((1, units), F32),
            pltpu.VMEM((1, units), F32),
            pltpu.VMEM((width - 1, rows, d), BF16),
            pltpu.VMEM((width - 1, rows, d), BF16),
            pltpu.VMEM((rows, d), F32),
            pltpu.VMEM((width, rows, d), BF16),
            pltpu.VMEM((width, rows, d), BF16),
            pltpu.VMEM((8, meta_lanes), F32),
            pltpu.VMEM((8, meta_lanes), F32),
            pltpu.VMEM((chips, rows, d), BF16),
            pltpu.VMEM((max(width, chips) * rows, d), F32),
            pltpu.VMEM((chips, rows, d), BF16),
            pltpu.VMEM((chips - 1, rows, d), BF16),
            pltpu.VMEM((rows, d), F32),
            dma((10,)),
            dma((ny,)),
        ]
        + [dma] * 12,
        compiler_params=pltpu.CompilerParams(
            collective_id=0, has_side_effects=True, vmem_limit_bytes=60 * 1024 * 1024
        ),
    )(tokens, counts, image_ids, gain, shift, w_up, w_down, text_rows, text_ids, scale, bias)


def local(
    geometry,
    image_tokens,
    image_counts,
    image_ids,
    norm_gain,
    norm_bias,
    up_weight,
    down_weight,
    text_rows,
    text_counts,
    text_ids,
    logit_scale,
    logit_bias,
):
    grads = fused(
        geometry,
        image_tokens,
        image_counts,
        image_ids.reshape(1, -1),
        norm_gain.reshape(1, -1),
        norm_bias.reshape(1, -1),
        up_weight,
        down_weight,
        text_rows,
        text_ids,
        logit_scale.reshape(1, 1),
        logit_bias.reshape(1, 1),
    )
    text_valid = (jnp.arange(text_rows.shape[0], dtype=jnp.int32) < text_counts[0]).astype(F32)
    return grads * text_valid[:, None]


def solution(mesh, geometry=GEOMETRY):
    placed = (
        P("dp", None, None),
        P("dp", None),
        P("dp"),
        P(),
        P(),
        P(None, "mp"),
        P("mp", None),
        P(("dp", "mp"), None),
        P(("dp", "mp")),
        P(),
        P(),
        P(),
    )
    return jax.shard_map(
        functools.partial(local, geometry),
        mesh=mesh,
        in_specs=placed,
        out_specs=P(("dp", "mp"), None),
        check_vma=False,
    )
```

time: 112 us -> 56.6 us (0.51)
  Pallas kernels: 0 us -> 50.4 us
  waiting for transfers between devices: 45.6 us -> 0 us
  starting transfers between devices: 44.9 us -> 0 us
  other arithmetic: 8.6 us -> 1.4 us
  matrix products: 4.54 us -> 0 us
  local copies, waits for them, and re-layouts: 5.57 us -> 2.58 us
    pallas_call x0 -> x1, Pallas kernels: none -> 50.4 us  [fused(): pl.pallas_call(functools.partial(kernel, geometry), out_shape=jax.ShapeDt...]
    all_to_all x4 -> x0, waiting for transfers between devices: 45.6 us -> none  [the longest x2 23.4 us: sum_at_owner(): tiles = lax.all_to_all(in_blocks(shard, dim, count), axis, 0, 0, tiled=True)]
    all_to_all x4 -> x0, starting transfers between devices: 44.9 us -> none  [the longest x2 25.9 us: copy_for_each(): lax.all_to_all(jnp.broadcast_to(shard[None], (count, *shard.shape)), axis...]
    reduce_sum x7 -> x0, other arithmetic: 7.72 us -> none  [the longest x1 4.15 us: layer_norm(): center = jnp.mean(values, axis=-1, keepdims=True)]
    dot_general x3 -> x0, matrix products: 4.54 us -> none  [the longest x1 3.72 us: local(): jnp.dot(normed, up_weight, preferred_element_type=jnp.float32)]
    broadcast_in_dim x2 -> x0, local copies, waits for them, and re-layouts: 1.52 us -> none  [copy_for_each(): jnp.broadcast_to(shard[None], (count, *shard.shape))]
    gather x1 -> x0, local copies, waits for them, and re-layouts: 1.23 us -> none  [local(): jnp.repeat(image_counts[0], rows_dev, total_repeat_length=group_rows)]
    reshape x5 -> x2, local copies, waits for them, and re-layouts: 1.72 us -> 2.58 us  [the longest x1 1.29 us: local(): norm_gain.reshape(1, -1)]
  transfers between devices with their start and end apart: 4 -> 0, of which waited for: 4 -> 0; matrix products, arithmetic and copies ran while one was open for 3% -> 0% of each run, Pallas kernels for 0% -> 0%
where the time goes in v1:
time: 56.6 us; the launch traced here: 56.3 us
  Pallas kernels  50.4 us (89%)
  local copies, waits for them, and re-layouts  2.58 us (5%)
  between operations  1.96 us (3%)
  other arithmetic  1.4 us (2%)
    pallas_call x1, Pallas kernels, fused(): pl.pallas_call(functools.partial(kernel, geometry), out_shape=jax.ShapeDt...  50.4 us
    mul x1, other arithmetic, local(): return grads * text_valid[:, None]  1.4 us
    reshape x1, local copies, waits for them, and re-layouts, local(): norm_gain.reshape(1, -1)  1.29 us
    reshape x1, local copies, waits for them, and re-layouts, local(): norm_bias.reshape(1, -1)  1.29 us

profile of v1, /device:TPU:1, one launch (start us, length us, event | category | flops | bytes accessed | tf_op | source)
XLA Modules:
  0.0 56.3 jit_solution(9107405063339565461)
XLA Ops:
  0.0 1.3 %reshape.21.gain = f32[1,1152]{1,0:T(1,128)} reshape(f32[1152]{0:T(1024)} %param.15) | data formatting | bytes 9216 | tf_op jit(solution)/shard_map/reshape | solution.py:401
  1.3 1.3 %reshape.22.shift = f32[1,1152]{1,0:T(1,128)} reshape(f32[1152]{0:T(1024)} %param.16) | data formatting | bytes 9216 | tf_op jit(solution)/shard_map/reshape | solution.py:402
  3.9 50.4 %shard_map.118 = f32[4,1152]{1,0:T(4,128)} custom-call(bf16[96,32,1152]{2,1,0:T(8,128)(2,1)} %tokens.1, s32[1,24]{1,0:T(1,128)} %counts.1, s32[1,96]{1,0:T(1,128)} %bitcast.7, f32[1,1152]{1,0:T(1,128)} %reshape.21.gain, f32[1,1152]{1,0:T(1,128)} %reshape.22.shift, bf16[1152,128]{1,0:T(8,128)(2,1)} %w_up.1, bf16[128,1152]{1,0:T(8,128)(2,1)} %w_down.1, ...), custom_call_target="tpu_custom_call" | custom-call | tf_op jit(solution)/shard_map/pallas_call | solution.py:339
  54.9 1.4 %broadcast_multiply_fusion = f32[4,1152]{1,0:T(4,128)} fusion(f32[4,1152]{1,0:T(4,128)} %shard_map.118, f32[4]{0:T(128)S(1)} %compare_convert_fusion), kind=kLoop, calls=%fused_computation | loop fusion | flops 4608 | bytes 36880 | tf_op jit(solution)/shard_map/mul | solution.py:411
  (1 shorter events, 0.0 us)

commit v2 on v1

v2 whole, which is shorter than its diff:
```python
import functools

import jax
import jax.numpy as jnp
from jax import lax
from jax.experimental import pallas as pl
from jax.experimental.pallas import tpu as pltpu
from jax.sharding import PartitionSpec as P

MESH = pl.DeviceIdType.MESH
EPS = 1e-06
F32 = jnp.float32
BF16 = jnp.bfloat16
GEOMETRY = (4, 4, 3, 8)
GELU_A = 0.7978845608028654
GELU_B = GELU_A * 0.044715
PAIR = 2
GREET = 1


def await_bytes(ref, sem):
    pltpu.make_async_copy(ref, ref, sem).wait()


def unit_rows(values):
    return values * lax.rsqrt(jnp.sum(values * values, axis=-1, keepdims=True) + EPS)


def gelu(u):
    half = 0.5 * u
    return half + half * jnp.tanh(u * (GELU_A + GELU_B * (u * u)))


def y_offset(step, ny):
    half = (step + 1) // 2
    return ny // 2 + half * (1 - 2 * (step % 2))


def kernel(
    geometry,
    tokens,
    counts,
    image_ids,
    gain,
    shift,
    w_up,
    w_down,
    text_rows,
    text_ids,
    scale,
    bias,
    out,
    x_buf,
    counts_v,
    ids_v,
    affine_v,
    up_v,
    down_v,
    text_v,
    text_ids_s,
    scale_s,
    bias_s,
    w_aug,
    pooled_v,
    part_send,
    part_recv,
    own_part,
    emb_own,
    emb_peer,
    meta_own,
    meta_peer,
    text_all,
    rows_f32,
    grad_send,
    grad_recv,
    own_grad,
    in_sem,
    x_sem,
    part_send_sem,
    part_recv_sem,
    emb_send_sem,
    emb_recv_sem,
    pair_send_sem,
    pair_recv_sem,
    meta_send_sem,
    meta_recv_sem,
    text_send_sem,
    text_recv_sem,
    grad_send_sem,
    grad_recv_sem,
):
    nx, nzh, nzl, ny = geometry
    width = nzl * ny
    chips = nx * nzh
    rows, d = text_rows.shape
    patches = tokens.shape[1]
    units = w_up.shape[1]
    group = width * rows
    lanes = d // 128
    dp = lax.axis_index("dp")
    mp = lax.axis_index("mp")
    core = dp % 2
    my_x = dp // (2 * nzh)
    my_zh = (dp // 2) % nzh
    my_zl = mp // ny
    my_y = mp % ny
    partner = dp + 1 - 2 * core
    my_chip = dp // 2

    def mp_of(y_off, z_off):
        return ((my_zl + z_off) % nzl) * ny + (my_y + y_off) % ny

    def dp_of(x_off, z_off):
        return (((my_x + x_off) % nx) * nzh + (my_zh + z_off) % nzh) * 2 + core

    mp_partners = [
        (y_off, z_off)
        for y_off in [y_offset(s, ny) for s in range(ny)]
        for z_off in [(z + 1) % nzl for z in range(nzl)]
    ][:-1]
    z_order = sorted(range(nzh), key=lambda o: -min(o, nzh - o))
    x_order = sorted(range(nx), key=lambda o: -min(o, nx - o))
    dp_partners = [(x_off, z_off) for z_off in z_order for x_off in x_order][:-1]

    small = [
        (w_up, up_v),
        (gain, affine_v.at[pl.ds(0, lanes)]),
        (shift, affine_v.at[pl.ds(16, lanes)]),
        (w_down, down_v),
        (text_rows, text_v),
        (counts, counts_v),
        (image_ids, ids_v),
        (text_ids, text_ids_s),
        (scale, scale_s),
        (bias, bias_s),
    ]
    for index, (source, target) in enumerate(small[:3]):
        pltpu.make_async_copy(source, target, in_sem.at[index]).start()

    def load(step, z_off):
        start = mp_of(y_offset(step, ny), z_off) * rows
        pltpu.make_async_copy(
            tokens.at[pl.ds(start, rows)], x_buf.at[step, pl.ds(z_off * rows, rows)], x_sem.at[step]
        ).start()

    def load_step(step):
        for z_off in range(nzl):
            load(step, z_off)

    load_step(0)
    barrier = pltpu.get_barrier_semaphore()
    for y_off, z_off in mp_partners:
        pl.semaphore_signal(barrier, inc=1, device_id=(dp, mp_of(y_off, z_off)), device_id_type=MESH)
    for x_off, z_off in dp_partners:
        pl.semaphore_signal(barrier, inc=1, device_id=(dp_of(x_off, z_off), mp), device_id_type=MESH)
    pl.semaphore_signal(barrier, inc=1, device_id=(partner, mp), device_id_type=MESH)

    for step in range(1, ny):
        load_step(step)
        if step == 1:
            for index, (source, target) in enumerate(small):
                if index >= 3:
                    pltpu.make_async_copy(source, target, in_sem.at[index]).start()
    for index in range(3):
        pltpu.make_async_copy(*small[index], in_sem.at[index]).wait()

    columns = jnp.transpose(affine_v[...])
    total = jnp.zeros((8, units), F32)
    moved = jnp.zeros((8, units), F32)
    for j in range(lanes):
        cut = pl.ds(j * 128, 128)
        block = up_v[cut, :].astype(F32)
        scaled = (block * columns[:, j : j + 1]).astype(BF16)
        w_aug[cut, pl.ds(0, units)] = scaled
        w_aug[cut, pl.ds(units, 128)] = jnp.ones((128, 128), BF16)
        total += jnp.sum(scaled.astype(F32).reshape(16, 8, units), axis=0)
        moved += jnp.sum((block * columns[:, 16 + j : 17 + j]).reshape(16, 8, units), axis=0)
    w_sum = jnp.sum(total, axis=0, keepdims=True)
    w_shift = jnp.sum(moved, axis=0, keepdims=True)

    meta_copy = pltpu.make_async_remote_copy(
        meta_own, meta_peer, meta_send_sem, meta_recv_sem, device_id=(partner, mp), device_id_type=MESH
    )

    def own_rows():
        for index in range(3, len(small)):
            pltpu.make_async_copy(*small[index], in_sem.at[index]).wait()

        text_all[my_chip] = unit_rows(text_v[...].astype(F32)).astype(BF16)
        slot = lax.broadcasted_iota(jnp.int32, (width, group), 1)
        owner = lax.broadcasted_iota(jnp.int32, (width, group), 0)
        spread = jnp.where(slot // rows == owner, 1.0, 0.0).astype(BF16)
        row_counts = jnp.dot(
            jnp.broadcast_to(counts_v[...].astype(F32), (8, width)).astype(BF16),
            spread,
            preferred_element_type=F32,
        )[:1]
        place = (lax.broadcasted_iota(jnp.int32, (1, group), 1) % rows).astype(F32)
        meta_own[pl.ds(0, 1), pl.ds(0, group)] = ids_v[...].astype(F32)
        meta_own[pl.ds(1, 1), pl.ds(0, group)] = jnp.where(place < row_counts, 1.0, 0.0)

    images = nzl * rows
    tokens_of = rows * patches

    def project(step):
        await_bytes(x_buf.at[step], x_sem.at[step])
        return jnp.dot(
            x_buf[step].reshape(images * patches, d), w_aug[...], preferred_element_type=F32
        )

    def pool(step, product):
        for z_off in range(nzl):
            part = product[z_off * tokens_of : (z_off + 1) * tokens_of]
            mean = part[:, units:] * (1.0 / d)
            near = mean.astype(BF16)
            wide = jnp.concatenate([near, near], axis=1)
            squares = jnp.zeros((tokens_of, 128), F32)
            for at in range(0, d, 256):
                size = min(256, d - at)
                piece = x_buf[step, pl.ds(z_off * rows, rows), :, pl.ds(at, size)]
                piece = piece.reshape(tokens_of, size) - wide[:, :size]
                square = (piece * piece).astype(F32)
                squares += square[:, :128]
                if size > 128:
                    squares += square[:, 128:]
            rest = mean[:, :1] - near[:, :1].astype(F32)
            spread_of = jnp.sum(squares, axis=-1, keepdims=True) * (1.0 / d) - rest * rest
            before = (part[:, :units] - mean * w_sum) * lax.rsqrt(spread_of + EPS) + w_shift
            hidden = gelu(before).astype(BF16).astype(F32)
            pooled_v[pl.ds(step * images + z_off * rows, rows), :] = jnp.sum(
                hidden.reshape(rows, patches, units), axis=1
            ) * (1.0 / patches)

    def slot_of(step, z_off):
        return step * nzl + (z_off + nzl - 1) % nzl

    def send(step):
        for z_off in [(z + 1) % nzl for z in range(nzl)]:
            if (step, z_off) != (ny - 1, 0):
                pltpu.make_async_remote_copy(
                    part_send.at[slot_of(step, z_off)],
                    part_recv.at[slot_of(step, z_off)],
                    part_send_sem,
                    part_recv_sem,
                    device_id=(dp, mp_of(y_offset(step, ny), z_off)),
                    device_id_type=MESH,
                ).start()

    product = project(0)
    for step in range(ny):
        following = project(step + 1) if step + 1 < ny else None
        pool(step, product)
        product = following
        if step % PAIR == PAIR - 1:
            first = step - PAIR + 1
            if first == 0:
                own_rows()
            part = jnp.dot(
                pooled_v[pl.ds(first * images, PAIR * images), :].astype(BF16),
                down_v[...],
                preferred_element_type=F32,
            )
            for done in range(first, step + 1):
                for z_off in range(nzl):
                    at = (done - first) * images + z_off * rows
                    term = part[at : at + rows]
                    if (done, z_off) == (ny - 1, 0):
                        own_part[...] = term
                    else:
                        part_send[slot_of(done, z_off)] = term.astype(BF16)
            ready = step // PAIR + 1
            if ready == GREET:
                pl.semaphore_wait(barrier, len(mp_partners) + len(dp_partners) + 1)
            if ready >= GREET:
                for done in range(0 if ready == GREET else first, step + 1):
                    send(done)
            if ready == GREET:
                meta_copy.start()
                for z_off in z_order[:-1]:
                    pltpu.make_async_remote_copy(
                        text_all.at[my_chip],
                        text_all.at[my_chip],
                        text_send_sem.at[0],
                        text_recv_sem.at[0],
                        device_id=(dp_of(0, z_off), mp),
                        device_id_type=MESH,
                    ).start()

    await_bytes(text_all.at[pl.ds(0, nzh - 1)], text_recv_sem.at[0])
    text_mine = text_all.at[pl.ds(my_x * nzh, nzh)]
    for x_off in x_order[:-1]:
        pltpu.make_async_remote_copy(
            text_mine,
            text_mine,
            text_send_sem.at[1],
            text_recv_sem.at[1],
            device_id=(dp_of(x_off, 0), mp),
            device_id_type=MESH,
        ).start()

    pooled_tokens = jnp.sum(x_buf[ny - 1, pl.ds(0, rows)].astype(F32), axis=1) * (1.0 / patches)
    tower = pooled_tokens + own_part[...]

    id_blocks = []
    lane_row = lax.broadcasted_iota(jnp.int32, (8, 128), 0)
    for start in range(0, chips * rows, 8):
        block = jnp.zeros((8, 128), jnp.int32)
        for k in range(8):
            chip, r = (start + k) // rows, (start + k) % rows
            entry = text_ids_s[((chip * 2 + core) * width + mp) * rows + r]
            block = jnp.where(lane_row == k, entry, block)
        id_blocks.append(block)
    id_column = jnp.concatenate(id_blocks, axis=0)[:, :group].astype(F32)

    await_bytes(part_recv, part_recv_sem)
    tower += jnp.sum(part_recv[...].astype(F32), axis=0)
    emb_own[mp] = unit_rows(tower).astype(BF16)
    for y_off, z_off in mp_partners:
        pltpu.make_async_remote_copy(
            emb_own.at[mp],
            emb_own.at[mp],
            emb_send_sem,
            emb_recv_sem,
            device_id=(dp, mp_of(y_off, z_off)),
            device_id_type=MESH,
        ).start()

    def flat(blocks_ref, count):
        for k in range(count):
            rows_f32[pl.ds(k * rows, rows), :] = blocks_ref[k].astype(F32)
        return rows_f32[pl.ds(0, count * rows), :].astype(BF16)

    if nx > 1:
        await_bytes(text_all.at[pl.ds(0, chips - nzh)], text_recv_sem.at[1])
    text_emb = flat(text_all, chips)
    meta_copy.wait_recv()

    def pair_terms(emb, meta):
        cosines = lax.dot_general(
            text_emb, emb, (((1,), (1,)), ((), ())), preferred_element_type=F32
        )
        logits = scale_s[0] * cosines + bias_s[0]
        same = id_column == meta[pl.ds(0, 1), pl.ds(0, group)]
        sign = jnp.where(same, 1.0, -1.0)
        weights = (
            meta[pl.ds(1, 1), pl.ds(0, group)] * -sign * jax.nn.sigmoid(-sign * logits) * scale_s[0]
        )
        return jnp.dot(weights.astype(BF16), emb, preferred_element_type=F32)

    await_bytes(emb_own.at[pl.ds(0, width - 1)], emb_recv_sem)
    pair_copy = pltpu.make_async_remote_copy(
        emb_own, emb_peer, pair_send_sem, pair_recv_sem, device_id=(partner, mp), device_id_type=MESH
    )
    pair_copy.start()
    grads = pair_terms(flat(emb_own, width), meta_own)
    pair_copy.wait_recv()
    grads += pair_terms(flat(emb_peer, width), meta_peer)

    for k in range(chips):
        grad_send[k] = grads[k * rows : (k + 1) * rows].astype(BF16)
    for index, (x_off, z_off) in enumerate(dp_partners):
        target = dp_of(x_off, z_off)
        pltpu.make_async_remote_copy(
            grad_send.at[target // 2],
            grad_recv.at[index],
            grad_send_sem,
            grad_recv_sem,
            device_id=(target, mp),
            device_id_type=MESH,
        ).start()
    own_grad[...] = grad_send[my_chip].astype(F32)

    await_bytes(part_send, part_send_sem)
    await_bytes(emb_own.at[pl.ds(0, width - 1)], emb_send_sem)
    await_bytes(text_all.at[pl.ds(0, nzh - 1)], text_send_sem.at[0])
    if nx > 1:
        await_bytes(text_all.at[pl.ds(0, chips - nzh)], text_send_sem.at[1])
    meta_copy.wait_send()
    pair_copy.wait_send()
    await_bytes(grad_send.at[pl.ds(0, chips - 1)], grad_send_sem)
    await_bytes(grad_recv, grad_recv_sem)
    out[...] = own_grad[...] + jnp.sum(grad_recv[...].astype(F32), axis=0)


def fused(geometry, tokens, counts, image_ids, gain, shift, w_up, w_down, text_rows, text_ids, scale, bias):
    nx, nzh, nzl, ny = geometry
    width, chips = nzl * ny, nx * nzh
    rows, d = text_rows.shape
    units = w_up.shape[1]
    patches = tokens.shape[1]
    group = width * rows
    meta_lanes = -(-group // 128) * 128
    dma = pltpu.SemaphoreType.DMA
    return pl.pallas_call(
        functools.partial(kernel, geometry),
        out_shape=pltpu.VMEM((rows, d), F32),
        in_specs=[pl.BlockSpec(memory_space=pltpu.HBM)] * 11,
        out_specs=pl.BlockSpec(memory_space=pltpu.VMEM),
        scratch_shapes=[
            pltpu.VMEM((ny, nzl * rows, patches, d), BF16),
            pltpu.VMEM(counts.shape, jnp.int32),
            pltpu.VMEM(image_ids.shape, jnp.int32),
            pltpu.VMEM((32, 128), F32),
            pltpu.VMEM(w_up.shape, BF16),
            pltpu.VMEM(w_down.shape, BF16),
            pltpu.VMEM(text_rows.shape, BF16),
            pltpu.SMEM(text_ids.shape, jnp.int32),
            pltpu.SMEM(scale.shape, F32),
            pltpu.SMEM(bias.shape, F32),
            pltpu.VMEM((d, units + 128), BF16),
            pltpu.VMEM((group, units), F32),
            pltpu.VMEM((width - 1, rows, d), BF16),
            pltpu.VMEM((width - 1, rows, d), BF16),
            pltpu.VMEM((rows, d), F32),
            pltpu.VMEM((width, rows, d), BF16),
            pltpu.VMEM((width, rows, d), BF16),
            pltpu.VMEM((8, meta_lanes), F32),
            pltpu.VMEM((8, meta_lanes), F32),
            pltpu.VMEM((chips, rows, d), BF16),
            pltpu.VMEM((max(width, chips) * rows, d), F32),
            pltpu.VMEM((chips, rows, d), BF16),
            pltpu.VMEM((chips - 1, rows, d), BF16),
            pltpu.VMEM((rows, d), F32),
            dma((10,)),
            dma((ny,)),
        ]
        + [dma] * 8
        + [dma((2,)), dma((2,)), dma, dma],
        compiler_params=pltpu.CompilerParams(
            collective_id=0, has_side_effects=True, vmem_limit_bytes=60 * 1024 * 1024
        ),
    )(tokens, counts, image_ids, gain, shift, w_up, w_down, text_rows, text_ids, scale, bias)


def local(
    geometry,
    image_tokens,
    image_counts,
    image_ids,
    norm_gain,
    norm_bias,
    up_weight,
    down_weight,
    text_rows,
    text_counts,
    text_ids,
    logit_scale,
    logit_bias,
):
    grads = fused(
        geometry,
        image_tokens,
        image_counts,
        image_ids.reshape(1, -1),
        norm_gain.reshape(-1, 128),
        norm_bias.reshape(-1, 128),
        up_weight,
        down_weight,
        text_rows,
        text_ids,
        logit_scale,
        logit_bias,
    )
    text_valid = (jnp.arange(text_rows.shape[0], dtype=jnp.int32) < text_counts[0]).astype(F32)
    return grads * text_valid[:, None]


def solution(mesh, geometry=GEOMETRY):
    placed = (
        P("dp", None, None),
        P("dp", None),
        P("dp"),
        P(),
        P(),
        P(None, "mp"),
        P("mp", None),
        P(("dp", "mp"), None),
        P(("dp", "mp")),
        P(),
        P(),
        P(),
    )
    return jax.shard_map(
        functools.partial(local, geometry),
        mesh=mesh,
        in_specs=placed,
        out_specs=P(("dp", "mp"), None),
        check_vma=False,
    )
```

time: 56.6 us -> 49.3 us (0.87)
  Pallas kernels: 50.4 us -> 46.5 us
  local copies, waits for them, and re-layouts: 2.58 us -> 0 us
  other arithmetic: 1.4 us -> 0.68 us
    pallas_call x1, Pallas kernels: 50.4 us -> 46.5 us  [fused(): pl.pallas_call(functools.partial(kernel, geometry), out_shape=pltpu.VMEM(...]
    reshape x2 -> x0, local copies, waits for them, and re-layouts: 2.58 us -> none  [the longest x1 1.29 us: local(): norm_gain.reshape(1, -1)]
    mul x1, other arithmetic: 1.4 us -> 0.68 us  [local(): return grads * text_valid[:, None]]
where the time goes in v2:
time: 49.3 us; the launch traced here: 49.1 us
  Pallas kernels  46.5 us (94%)
  between operations  1.96 us (4%)
  other arithmetic  0.68 us (1%)
    pallas_call x1, Pallas kernels, fused(): pl.pallas_call(functools.partial(kernel, geometry), out_shape=pltpu.VMEM(...  46.5 us

profile of v2, /device:TPU:1, one launch (start us, length us, event | category | flops | bytes accessed | tf_op | source)
XLA Modules:
  0.0 49.1 jit_solution(4380297479133095218)
XLA Ops:
  1.3 46.5 %shard_map.118 = f32[4,1152]{1,0:T(4,128)S(1)} custom-call(bf16[96,32,1152]{2,1,0:T(8,128)(2,1)} %tokens.1, s32[1,24]{1,0:T(1,128)} %counts.1, s32[1,96]{1,0:T(1,128)} %bitcast.7, f32[9,128]{1,0:T(8,128)} %bitcast.5, f32[9,128]{1,0:T(8,128)} %bitcast.6, bf16[1152,128]{1,0:T(8,128)(2,1)} %w_up.1, bf16[128,1152]{1,0:T(8,128)(2,1)} %w_down.1, ...), custom_call_target="tpu_custom_call" | custom-call | tf_op jit(solution)/shard_map/pallas_call | solution.py:394
  48.4 0.7 %broadcast_multiply_fusion = f32[4,1152]{1,0:T(4,128)} fusion(f32[4,1152]{1,0:T(4,128)S(1)} %shard_map.118, f32[4]{0:T(128)S(1)} %compare_convert_fusion), kind=kLoop, calls=%fused_computation | loop fusion | flops 4608 | bytes 36880 | tf_op jit(solution)/shard_map/mul | solution.py:465
  (1 shorter events, 0.0 us)
